TPU v7x, 256 devices: a whole 4x4x8 slice. The times are simulated.
256 devices in a mesh: slab: 128 (over y, z, x), energy: 2 (over core).
Axes of the slice: x: 4, y: 4, z: 8, core: 2. Of those that a mesh axis runs over, the one named last changes fastest.
Arguments:
- onsite_energy: float32 [256, 128], P('slab'), may hold values from -0.3 to 0.3
- onsite_mixing: float32 [256, 128, 128], P('slab'), may hold values from -0.15625 to 0.15625
- hop_strength: float32 [256, 128], P('slab'), may hold values from 0.8 to 1.2
- hop_mixing: float32 [256, 128, 128], P('slab'), may hold values from -0.15625 to 0.15625
- energy: float32 [2], P('energy'), parts along dimension 0, may hold values from -0.4 to 0.4
- broadening: float32 [2], P('energy'), parts along dimension 0, may hold values from 0.01 to 0.025
Outputs:
- green_real: float32 [512, 128, 128], P(('energy', 'slab')), parts along dimension 0
- green_imag: float32 [512, 128, 128], P(('energy', 'slab')), parts along dimension 0
There are 2 independent parts, one for each index of `energy`. A program takes and returns all parts, laid end to end along the dimension named above; an argument that names none is the same for every part. Nothing has to cross between parts.
All inputs are finite; a program needn't handle non-finite values.
Results may differ from a plain program's by a relative error of at most 0.0007.
Values sent between devices are 32-bit elements; how exact they have to be, the bound alone decides.
A program may use at most 128 MiB of HBM per device.

v0:
```python
import functools

import jax
import jax.numpy as jnp
from jax import lax
from jax.experimental import pallas as pl
from jax.experimental.pallas import tpu as pltpu
from jax.sharding import PartitionSpec as P

MESH = pl.DeviceIdType.MESH
F32 = jnp.float32
STRIP = 8


def times(a, b):
    return a[0] * b[0] - a[1] * b[1], a[0] * b[1] + a[1] * b[0]


def minus(a, b):
    return a[0] - b[0], a[1] - b[1]


def select(mask, a, b):
    return jnp.where(mask, a[0], b[0]), jnp.where(mask, a[1], b[1])


def row_of(x, j):
    return tuple(jnp.broadcast_to(v[j : j + 1, :], v.shape) for v in x)


def lane_of(x, lanes):
    return tuple(jnp.take_along_axis(v, lanes, axis=1) for v in x)


def dot(a, b, transpose_b=False):
    dims = (((1,), (1 if transpose_b else 0,)), ((), ()))
    return lax.dot_general(a, b, dims, precision=lax.Precision.HIGHEST, preferred_element_type=F32)


def beside(x):
    return jnp.concatenate([x[0], x[1]], axis=1)


def square(x):
    top = jnp.concatenate([x[0], x[1]], axis=1)
    return jnp.concatenate([top, jnp.concatenate([-x[1], x[0]], axis=1)], axis=0)


def square_t(x):
    top = jnp.concatenate([x[0], -x[1]], axis=1)
    return jnp.concatenate([top, jnp.concatenate([x[1], x[0]], axis=1)], axis=0)


def halves(x):
    n = x.shape[1] // 2
    return x[:, :n], x[:, n:]


def cdot(a, b):
    return halves(dot(beside(a), square(b)))


def cdot_t(a, b):
    return halves(dot(beside(a), square_t(b), transpose_b=True))


def eliminated(rows, col_lanes, in_strip, sub, lane, first):
    columns = [lane_of(rows, lanes) for lanes in col_lanes]
    eye = jnp.where(lane - first == sub, 1.0, 0.0)
    rows = select(in_strip, (eye, jnp.zeros_like(eye)), rows)
    for j in range(STRIP):
        own = sub == j
        factor = columns[j]
        pivot = row_of(factor, j)
        scale = 1.0 / (pivot[0] * pivot[0] + pivot[1] * pivot[1])
        inverse = (pivot[0] * scale, -pivot[1] * scale)
        for k in range(j + 1, STRIP):
            entry = row_of(columns[k], j)
            columns[k] = select(
                own,
                times(entry, inverse),
                minus(columns[k], times(times(factor, entry), inverse)),
            )
        entry = row_of(rows, j)
        rows = select(
            own, times(entry, inverse), minus(rows, times(times(factor, inverse), entry))
        )
    return rows


def invert(mats):
    n = mats[0][0].shape[0]
    strips = n // STRIP
    lane = lax.broadcasted_iota(jnp.int32, (STRIP, n), 1)
    sub = lax.broadcasted_iota(jnp.int32, (STRIP, n), 0)
    zero = jnp.zeros((STRIP, n), F32)

    def lanes_of(step):
        return [jnp.full((STRIP, n), step * STRIP + j, jnp.int32) for j in range(STRIP)]

    def updated(x, lanes, in_strip, pivots):
        columns = [lane_of(x, ids) for ids in lanes]
        x = select(in_strip, (zero, zero), x)
        for j in range(STRIP):
            x = minus(x, times(columns[j], pivots[j]))
        return x

    def trail(mat, step, lanes, in_strip, strip, pivots):
        for i in range(strips):
            rows = slice(i * STRIP, (i + 1) * STRIP)
            x = updated((mat[0][rows, :], mat[1][rows, :]), lanes, in_strip, pivots)
            x = select(jnp.full((STRIP, n), i == step), strip, x)
            mat[0][rows, :] = x[0]
            mat[1][rows, :] = x[1]

    def body(step, carry):
        lanes_before, lanes = lanes_of(jnp.maximum(step - 1, 0)), lanes_of(step)
        in_before, in_strip = lane // STRIP == step - 1, lane // STRIP == step
        ahead = pl.multiple_of(jnp.minimum(step + 1, strips - 1) * STRIP, STRIP)
        out = []
        for mat, (rows, before) in zip(mats, carry):
            pivots = [row_of(before, j) for j in range(STRIP)]
            following = (mat[0][pl.ds(ahead, STRIP), :], mat[1][pl.ds(ahead, STRIP), :])
            following = updated(following, lanes_before, in_before, pivots)
            columns = [lane_of(following, ids) for ids in lanes]
            following = select(in_strip, (zero, zero), following)
            trail(mat, step - 1, lanes_before, in_before, before, pivots)
            rows = eliminated(rows, lanes, in_strip, sub, lane, step * STRIP)
            for j in range(STRIP):
                following = minus(following, times(columns[j], row_of(rows, j)))
            out.append((following, rows))
        return tuple(out)

    start = tuple(
        ((mat[0][0:STRIP, :], mat[1][0:STRIP, :]), (zero, zero)) for mat in mats
    )
    last = lax.fori_loop(0, strips, body, start)
    for mat, (_, strip) in zip(mats, last):
        pivots = [row_of(strip, j) for j in range(STRIP)]
        trail(mat, strips - 1, lanes_of(strips - 1), lane // STRIP == strips - 1, strip, pivots)


def packed(x, row, col):
    diagonal = jnp.sum(jnp.where(row == col, x[1], 0.0), axis=0, keepdims=True)
    mean = 0.5 * (jnp.where(row >= col, x[0], x[1]) + jnp.where(row <= col, x[0], x[1]).T)
    return mean, jnp.broadcast_to(diagonal, (STRIP, x[0].shape[1]))


def unpacked(ref, row, col):
    n = ref.shape[1]
    body = ref[0:n, :]
    other = body.T
    diagonal = jnp.broadcast_to(ref[n : n + 1, :], (n, n))
    real = jnp.where(row >= col, body, other)
    imag = jnp.where(row < col, body, jnp.where(row > col, other, diagonal))
    return real, imag


def kernel(
    count, onsite_ref, mixing_ref, strength_ref, hopping_ref, energy_ref, broadening_ref,
    real_ref, imag_ref,
    own_ref, low_ref, high_ref, work, spare,
    packed_out, packed_low, packed_high, link_low, link_high, from_low, from_high, strength_low,
    pack_up_send, pack_up_recv, pack_down_send, pack_down_recv,
    link_up_send, link_up_recv, link_down_send, link_down_recv, raw_send, raw_recv,
):
    levels = count.bit_length() - 1
    last = levels + 1
    n = mixing_ref.shape[1]
    me = lax.axis_index("slab")
    row = lax.broadcasted_iota(jnp.int32, (n, n), 0)
    col = lax.broadcasted_iota(jnp.int32, (n, n), 1)
    broadening = jnp.where(row == col, broadening_ref[0], 0.0)

    def diagonal(values):
        return jnp.where(row == col, jnp.broadcast_to(values, (n, n)), 0.0)

    def onsite(index):
        mixing = mixing_ref[index]
        hamilton = diagonal(onsite_ref[index : index + 1, :]) + 0.5 * (mixing + mixing.T)
        return jnp.where(row == col, energy_ref[0], 0.0) - hamilton

    def coupling(strengths, hoppings, index):
        return diagonal(strengths[index : index + 1, :]) + hoppings[index]

    def copy(source, target, send, recv, slab):
        return pltpu.make_async_remote_copy(
            src_ref=source, dst_ref=target, send_sem=send, recv_sem=recv,
            device_id={"slab": slab}, device_id_type=MESH,
        )

    def pack_up(slot, slab):
        return copy(packed_out.at[slot], packed_low.at[slot], pack_up_send.at[slot],
                    pack_up_recv.at[slot], slab)

    def pack_down(slot, slab):
        return copy(packed_out.at[slot], packed_high.at[slot], pack_down_send.at[slot],
                    pack_down_recv.at[slot], slab)

    def link_up(slot, slab):
        return copy(link_low.at[slot], from_low.at[slot], link_up_send.at[slot],
                    link_up_recv.at[slot], slab)

    def link_down(slot, slab):
        return copy(link_high.at[slot], from_high.at[slot], link_down_send.at[slot],
                    link_down_recv.at[slot], slab)

    def raw_mixing(slab):
        return copy(hopping_ref, from_low.at[0], raw_send.at[0], raw_recv.at[0], slab)

    def raw_strength(slab):
        return copy(strength_ref, strength_low, raw_send.at[1], raw_recv.at[1], slab)

    def pack(slot, value):
        square_part, tail_part = packed(value, row, col)
        packed_out[slot, 0:n, :] = square_part
        packed_out[slot, n : n + STRIP, :] = tail_part

    def set_work(refs, real):
        refs[0][...] = real
        refs[1][...] = broadening

    first = (work.at[0], work.at[1])
    second = (spare.at[0], spare.at[1])

    barrier = pltpu.get_barrier_semaphore()
    for level in range(levels):
        stride = 1 << level

        @pl.when(me >= stride)
        def _():
            pl.semaphore_signal(
                barrier, inc=1, device_id={"slab": me - stride}, device_id_type=MESH
            )

        @pl.when(me + stride < count)
        def _():
            pl.semaphore_signal(
                barrier, inc=1, device_id={"slab": me + stride}, device_id_type=MESH
            )

    peers = 0
    for level in range(levels):
        stride = 1 << level
        peers += (me >= stride).astype(jnp.int32) + (me + stride < count).astype(jnp.int32)
    pl.semaphore_wait(barrier, peers)

    @pl.when(me + 1 < count)
    def _():
        raw_mixing(me + 1).start()
        raw_strength(me + 1).start()

    @pl.when(me < 1)
    def _():
        from_low[0] = jnp.zeros((2, n, n), F32)
        strength_low[...] = jnp.zeros((2, n), F32)
        packed_low[0] = jnp.zeros((n + STRIP, n), F32)

    own_ref[...] = onsite(0)
    set_work(first, onsite(1))
    invert((first,))
    pack(0, (first[0][...], first[1][...]))

    @pl.when(me + 1 < count)
    def _():
        pack_up(0, me + 1).start()

    near = coupling(strength_ref, hopping_ref, 0)
    far = jnp.where(me < count - 1, coupling(strength_ref, hopping_ref, 1), 0.0)
    weight = halves(dot(near, beside(unpacked(packed_out.at[0], row, col))))
    both = jnp.concatenate([weight[0], weight[1]], axis=0)
    result = dot(both, near, transpose_b=True)
    high_ref[0] = result[:n]
    high_ref[1] = result[n:]
    result = dot(both, far)
    link_high[1, 0] = -result[:n]
    link_high[1, 1] = -result[n:]

    @pl.when(me >= 1)
    def _():
        raw_mixing(me).wait_recv()
        raw_strength(me).wait_recv()
        pack_up(0, me).wait_recv()

    near = coupling(strength_low, from_low.at[0], 0)
    far = coupling(strength_low, from_low.at[0], 1)
    weight = halves(dot(far.T, beside(unpacked(packed_low.at[0], row, col))))
    both = jnp.concatenate([weight[0], weight[1]], axis=0)
    result = dot(both, far)
    low_ref[0] = result[:n]
    low_ref[1] = result[n:]
    result = dot(both, near, transpose_b=True)
    link_low[1, 0] = -result[:n]
    link_low[1, 1] = -result[n:]

    def level_step(level, stride):
        has_low = me >= stride
        has_high = me + stride < count

        @pl.when(jnp.logical_and(level < levels, has_high))
        def _():
            link_up(level, me + stride).start()

        @pl.when(jnp.logical_and(level < levels, has_low))
        def _():
            link_down(level, me - stride).start()

        first[0][...] = own_ref[...] - low_ref[0] - high_ref[0]
        first[1][...] = broadening - low_ref[1] - high_ref[1]
        invert((first,))
        pack(level, (first[0][...], first[1][...]))

        @pl.when(has_high)
        def _():
            pack_up(level, me + stride).start()

        @pl.when(has_low)
        def _():
            pack_down(level, me - stride).start()

        @pl.when(jnp.logical_not(has_low))
        def _():
            from_low[level] = jnp.zeros((2, n, n), F32)
            packed_low[level] = jnp.zeros((n + STRIP, n), F32)

        @pl.when(jnp.logical_not(has_high))
        def _():
            from_high[level] = jnp.zeros((2, n, n), F32)
            packed_high[level] = jnp.zeros((n + STRIP, n), F32)

        @pl.when(has_low)
        def _():
            pack_up(level, me - stride).wait_recv()

        @pl.when(has_high)
        def _():
            pack_down(level, me + stride).wait_recv()

        low = (link_low[level, 0], link_low[level, 1])
        high = (link_high[level, 0], link_high[level, 1])
        low_weight = cdot(low, unpacked(packed_low.at[level], row, col))
        high_weight = cdot(high, unpacked(packed_high.at[level], row, col))
        term = cdot_t(low_weight, low)
        low_ref[0] += term[0]
        low_ref[1] += term[1]
        term = cdot_t(high_weight, high)
        high_ref[0] += term[0]
        high_ref[1] += term[1]

        @pl.when(level < levels)
        def _():
            @pl.when(has_low)
            def _():
                link_up(level, me - stride).wait_recv()

            @pl.when(has_high)
            def _():
                link_down(level, me + stride).wait_recv()

            term = cdot(low_weight, (from_low[level, 0], from_low[level, 1]))
            link_low[level + 1, 0] = -term[0]
            link_low[level + 1, 1] = -term[1]
            term = cdot(high_weight, (from_high[level, 0], from_high[level, 1]))
            link_high[level + 1, 0] = -term[0]
            link_high[level + 1, 1] = -term[1]

        return stride * 2

    lax.fori_loop(1, levels + 1, level_step, 1)

    first[0][...] = own_ref[...] - high_ref[0]
    first[1][...] = broadening - high_ref[1]
    second[0][...] = own_ref[...] - low_ref[0]
    second[1][...] = broadening - low_ref[1]
    invert((first, second))
    pack(last, (first[0][...], first[1][...]))

    @pl.when(me >= 1)
    def _():
        pack_down(last, me - 1).start()

    @pl.when(me + 1 >= count)
    def _():
        packed_high[last] = jnp.zeros((n + STRIP, n), F32)

    first[0][...] = own_ref[...] - low_ref[0] - high_ref[0]
    first[1][...] = broadening - low_ref[1] - high_ref[1]
    invert((first,))
    real_ref[0] = first[0][...]
    imag_ref[0] = first[1][...]

    near = coupling(strength_ref, hopping_ref, 0)
    far = jnp.where(me < count - 1, coupling(strength_ref, hopping_ref, 1), 0.0)
    mean = [0.5 * (ref[...] + ref[...].T) for ref in second]
    weight = halves(dot(near.T, beside(mean)))
    below = dot(jnp.concatenate([weight[0], weight[1]], axis=0), near)

    @pl.when(me + 1 < count)
    def _():
        pack_down(last, me + 1).wait_recv()

    weight = halves(dot(far, beside(unpacked(packed_high.at[last], row, col))))
    above = dot(jnp.concatenate([weight[0], weight[1]], axis=0), far, transpose_b=True)
    first[0][...] = onsite(1) - below[:n] - above[:n]
    first[1][...] = broadening - below[n:] - above[n:]
    invert((first,))
    real_ref[1] = first[0][...]
    imag_ref[1] = first[1][...]

    @pl.when(me + 1 < count)
    def _():
        raw_mixing(me + 1).wait_send()
        raw_strength(me + 1).wait_send()
        pack_up(0, me + 1).wait_send()

    @pl.when(me >= 1)
    def _():
        pack_down(last, me - 1).wait_send()

    def drain(level, stride):
        has_low = me >= stride
        has_high = me + stride < count

        @pl.when(has_high)
        def _():
            pack_up(level, me + stride).wait_send()

        @pl.when(has_low)
        def _():
            pack_down(level, me - stride).wait_send()

        @pl.when(jnp.logical_and(level < levels, has_high))
        def _():
            link_up(level, me + stride).wait_send()

        @pl.when(jnp.logical_and(level < levels, has_low))
        def _():
            link_down(level, me - stride).wait_send()

        return stride * 2

    lax.fori_loop(1, levels + 1, drain, 1)


def solution(mesh):
    count = mesh.shape["slab"]
    levels = count.bit_length() - 1

    def shards(onsite_energy, onsite_mixing, hop_strength, hop_mixing, energy, broadening):
        n = onsite_mixing.shape[1]
        whole = pl.BlockSpec(memory_space=pltpu.VMEM)
        scalar = pl.BlockSpec(memory_space=pltpu.SMEM)
        pair = jax.ShapeDtypeStruct((2, n, n), F32)
        pack_shape = pltpu.VMEM((levels + 2, n + STRIP, n), F32)
        link_shape = pltpu.VMEM((levels + 1, 2, n, n), F32)
        sems = pltpu.SemaphoreType.DMA((levels + 2,))
        return pl.pallas_call(
            functools.partial(kernel, count),
            out_shape=(pair, pair),
            in_specs=[whole] * 4 + [scalar] * 2,
            out_specs=(whole, whole),
            scratch_shapes=[
                pltpu.VMEM((n, n), F32),
                pltpu.VMEM((2, n, n), F32),
                pltpu.VMEM((2, n, n), F32),
                pltpu.VMEM((2, n, n), F32),
                pltpu.VMEM((2, n, n), F32),
                pack_shape, pack_shape, pack_shape,
                link_shape, link_shape, link_shape, link_shape,
                pltpu.VMEM((2, n), F32),
            ]
            + [sems] * 8
            + [pltpu.SemaphoreType.DMA((2,))] * 2,
            compiler_params=pltpu.CompilerParams(
                collective_id=0, has_side_effects=True, vmem_limit_bytes=40 * 1024 * 1024
            ),
        )(onsite_energy, onsite_mixing, hop_strength, hop_mixing, energy, broadening)

    return jax.shard_map(
        shards,
        mesh=mesh,
        in_specs=(
            P("slab", None),
            P("slab", None, None),
            P("slab", None),
            P("slab", None, None),
            P("energy"),
            P("energy"),
        ),
        out_specs=(P(("energy", "slab"), None, None), P(("energy", "slab"), None, None)),
        check_vma=False,
    )
```

profile of v0, /device:TPU:34, one launch (start us, length us, event | category | flops | bytes accessed | tf_op | source)
XLA Modules:
  0.0 233.3 jit_solution(1996913572698311199)
XLA Ops:
  0.6 0.0 copy-start.3
  1.3 0.0 copy-start.2
  2.0 0.0 copy-done.3
  2.0 0.0 copy-done.2
  2.0 0.0 copy-start
  2.0 0.9 copy-done
  2.9 0.0 copy-start.1
  2.9 0.9 copy-done.1
  3.8 228.2 %shard_map.77 = (f32[2,128,128]{2,1,0:T(8,128)S(1)}, f32[2,128,128]{2,1,0:T(8,128)S(1)}) custom-call(f32[2,128]{1,0:T(2,128)S(1)} %copy-done.2, f32[2,128,128]{2,1,0:T(8,128)S(1)} %copy-done, f32[2,128]{1,0:T(2,128)S(1)} %copy-done.3, f32[2,128,128]{2,1,0:T(8,128)S(1)} %copy-done.1, f32[1]{0:T(128)S(6)} %copy.10.energy_ref, f32[1]{0:T(128)S(6)} %copy.11.broadening_ref), custom_call_target="tpu_custom_call" | custom-call | tf_op jit(solution)/shard_map/pallas_call | solution.py:457
  232.0 0.7 copy.12
  232.7 0.7 copy.13
Async XLA Ops:
  0.6 1.3 copy-start.3
  1.3 0.7 copy-start.2
  2.0 0.9 copy-start
  2.9 0.9 copy-start.1
where the time goes:
time: 237 us; the launch traced here: 233 us
  Pallas kernels  228 us (96%)
  local copies, waits for them, and re-layouts  3.12 us (1%)
    pallas_call x1, Pallas kernels, shards(): pl.pallas_call(functools.partial(kernel, count), out_shape=(pair, pair),...  228 us

commit v1 on v0

--- a/solution.py
+++ b/solution.py
@@ -10,6 +10,7 @@
 MESH = pl.DeviceIdType.MESH
 F32 = jnp.float32
 STRIP = 8
+PANEL = 32
 
 
 def times(a, b):
@@ -28,8 +29,8 @@
     return tuple(jnp.broadcast_to(v[j : j + 1, :], v.shape) for v in x)
 
 
-def lane_of(x, lanes):
-    return tuple(jnp.take_along_axis(v, lanes, axis=1) for v in x)
+def lane_of(x, k):
+    return tuple(jnp.broadcast_to(v[:, k : k + 1], v.shape) for v in x)
 
 
 def dot(a, b, transpose_b=False):
@@ -64,80 +65,66 @@
     return halves(dot(beside(a), square_t(b), transpose_b=True))
 
 
-def eliminated(rows, col_lanes, in_strip, sub, lane, first):
-    columns = [lane_of(rows, lanes) for lanes in col_lanes]
+def eliminated(rows, columns, first, sub, lane):
+    zero = jnp.zeros_like(rows[0])
     eye = jnp.where(lane - first == sub, 1.0, 0.0)
-    rows = select(in_strip, (eye, jnp.zeros_like(eye)), rows)
+    rows = select((lane >= first) & (lane < first + STRIP), (eye, zero), rows)
     for j in range(STRIP):
         own = sub == j
         factor = columns[j]
         pivot = row_of(factor, j)
         scale = 1.0 / (pivot[0] * pivot[0] + pivot[1] * pivot[1])
         inverse = (pivot[0] * scale, -pivot[1] * scale)
-        for k in range(j + 1, STRIP):
-            entry = row_of(columns[k], j)
-            columns[k] = select(
-                own,
-                times(entry, inverse),
-                minus(columns[k], times(times(factor, entry), inverse)),
+        if j + 1 < STRIP:
+            entry = row_of(columns[j + 1], j)
+            change = select(own, (-entry[0], -entry[1]), times(factor, entry))
+            columns[j + 1] = minus(
+                select(own, (zero, zero), columns[j + 1]), times(change, inverse)
             )
-        entry = row_of(rows, j)
-        rows = select(
-            own, times(entry, inverse), minus(rows, times(times(factor, inverse), entry))
-        )
+        factor = select(own, (-inverse[0], -inverse[1]), times(factor, inverse))
+        for k in range(j + 2, STRIP):
+            change = times(factor, row_of(columns[k], j))
+            columns[k] = minus(select(own, (zero, zero), columns[k]), change)
+        rows = minus(select(own, (zero, zero), rows), times(factor, row_of(rows, j)))
     return rows
+
+
+def swept(strips, start, sub, lane):
+    zero = jnp.zeros_like(strips[0][0])
+    count = len(strips)
+    for s in range(count):
+        first = start + s * STRIP
+        columns = [[lane_of(x, first + j) for j in range(STRIP)] for x in strips]
+        done = eliminated(strips[s], columns[s], first, sub, lane)
+        pivots = [row_of(done, j) for j in range(STRIP)]
+        here = (lane >= first) & (lane < first + STRIP)
+        for step in range(1, count):
+            i = (s + step) % count
+            x = select(here, (zero, zero), strips[i])
+            for j in range(STRIP):
+                x = minus(x, times(columns[i][j], pivots[j]))
+            strips[i] = x
+        strips[s] = done
+    return strips
 
 
 def invert(mats):
     n = mats[0][0].shape[0]
-    strips = n // STRIP
     lane = lax.broadcasted_iota(jnp.int32, (STRIP, n), 1)
     sub = lax.broadcasted_iota(jnp.int32, (STRIP, n), 0)
-    zero = jnp.zeros((STRIP, n), F32)
-
-    def lanes_of(step):
-        return [jnp.full((STRIP, n), step * STRIP + j, jnp.int32) for j in range(STRIP)]
-
-    def updated(x, lanes, in_strip, pivots):
-        columns = [lane_of(x, ids) for ids in lanes]
-        x = select(in_strip, (zero, zero), x)
-        for j in range(STRIP):
-            x = minus(x, times(columns[j], pivots[j]))
-        return x
-
-    def trail(mat, step, lanes, in_strip, strip, pivots):
-        for i in range(strips):
-            rows = slice(i * STRIP, (i + 1) * STRIP)
-            x = updated((mat[0][rows, :], mat[1][rows, :]), lanes, in_strip, pivots)
-            x = select(jnp.full((STRIP, n), i == step), strip, x)
-            mat[0][rows, :] = x[0]
-            mat[1][rows, :] = x[1]
-
-    def body(step, carry):
-        lanes_before, lanes = lanes_of(jnp.maximum(step - 1, 0)), lanes_of(step)
-        in_before, in_strip = lane // STRIP == step - 1, lane // STRIP == step
-        ahead = pl.multiple_of(jnp.minimum(step + 1, strips - 1) * STRIP, STRIP)
-        out = []
-        for mat, (rows, before) in zip(mats, carry):
-            pivots = [row_of(before, j) for j in range(STRIP)]
-            following = (mat[0][pl.ds(ahead, STRIP), :], mat[1][pl.ds(ahead, STRIP), :])
-            following = updated(following, lanes_before, in_before, pivots)
-            columns = [lane_of(following, ids) for ids in lanes]
-            following = select(in_strip, (zero, zero), following)
-            trail(mat, step - 1, lanes_before, in_before, before, pivots)
-            rows = eliminated(rows, lanes, in_strip, sub, lane, step * STRIP)
-            for j in range(STRIP):
-                following = minus(following, times(columns[j], row_of(rows, j)))
-            out.append((following, rows))
-        return tuple(out)
-
-    start = tuple(
-        ((mat[0][0:STRIP, :], mat[1][0:STRIP, :]), (zero, zero)) for mat in mats
-    )
-    last = lax.fori_loop(0, strips, body, start)
-    for mat, (_, strip) in zip(mats, last):
-        pivots = [row_of(strip, j) for j in range(STRIP)]
-        trail(mat, strips - 1, lanes_of(strips - 1), lane // STRIP == strips - 1, strip, pivots)
+    wide = lax.broadcasted_iota(jnp.int32, (n, n), 1)
+    for start in range(0, n, PANEL):
+        stop = start + PANEL
+        here = (wide >= start) & (wide < stop)
+        for mat in mats:
+            strips = [tuple(r[a : a + STRIP, :] for r in mat) for a in range(start, stop, STRIP)]
+            strips = swept(strips, start, sub, lane)
+            panel = [jnp.concatenate([x[c] for x in strips], axis=0) for c in (0, 1)]
+            left = jnp.concatenate([r[:, start:stop] for r in mat], axis=1)
+            change = halves(dot(left, square(panel)))
+            for c in (0, 1):
+                mat[c][...] = jnp.where(here, 0.0, mat[c][...]) - change[c]
+                mat[c][start:stop, :] = panel[c]
 
 
 def packed(x, row, col):

time: 237 us -> 150 us (0.63)
  Pallas kernels: 228 us -> 142 us
    pallas_call x1, Pallas kernels: 228 us -> 142 us  [shards(): pl.pallas_call(functools.partial(kernel, count), out_shape=(pair, pair),...]
where the time goes in v1:
time: 150 us; the launch traced here: 147 us
  Pallas kernels  142 us (95%)
  local copies, waits for them, and re-layouts  3.12 us (2%)
  between operations  2 us (1%)
    pallas_call x1, Pallas kernels, shards(): pl.pallas_call(functools.partial(kernel, count), out_shape=(pair, pair),...  142 us
    unnamed x10, local copies, waits for them, and re-layouts  3.12 us

profile of v1, /device:TPU:34, one launch (start us, length us, event | category | flops | bytes accessed | tf_op | source)
XLA Modules:
  0.0 147.2 jit_solution(6470101612986093352)
XLA Ops:
  0.6 0.0 copy-start.3
  1.3 0.0 copy-start.2
  2.0 0.0 copy-done.3
  2.0 0.0 copy-done.2
  2.0 0.0 copy-start
  2.0 0.9 copy-done
  2.9 0.0 copy-start.1
  2.9 0.9 copy-done.1
  3.8 142.1 %shard_map.77 = (f32[2,128,128]{2,1,0:T(8,128)S(1)}, f32[2,128,128]{2,1,0:T(8,128)S(1)}) custom-call(f32[2,128]{1,0:T(2,128)S(1)} %copy-done.2, f32[2,128,128]{2,1,0:T(8,128)S(1)} %copy-done, f32[2,128]{1,0:T(2,128)S(1)} %copy-done.3, f32[2,128,128]{2,1,0:T(8,128)S(1)} %copy-done.1, f32[1]{0:T(128)S(6)} %copy.10.energy_ref, f32[1]{0:T(128)S(6)} %copy.11.broadening_ref), custom_call_target="tpu_custom_call" | custom-call | tf_op jit(solution)/shard_map/pallas_call | solution.py:444
  145.9 0.7 copy.12
  146.5 0.7 copy.13
Async XLA Ops:
  0.6 1.3 copy-start.3
  1.3 0.7 copy-start.2
  2.0 0.9 copy-start
  2.9 0.9 copy-start.1

commit v2 on v1

--- a/solution.py
+++ b/solution.py
@@ -30,7 +30,8 @@
 
 
 def lane_of(x, k):
-    return tuple(jnp.broadcast_to(v[:, k : k + 1], v.shape) for v in x)
+    lanes = jnp.full(x[0].shape, k, jnp.int32)
+    return tuple(jnp.take_along_axis(v, lanes, axis=1) for v in x)
 
 
 def dot(a, b, transpose_b=False):
@@ -108,23 +109,48 @@
     return strips
 
 
+def thirds(x):
+    high = x.astype(jnp.bfloat16)
+    rest = x - high.astype(F32)
+    middle = rest.astype(jnp.bfloat16)
+    return high, middle, (rest - middle.astype(F32)).astype(jnp.bfloat16)
+
+
 def invert(mats):
     n = mats[0][0].shape[0]
     lane = lax.broadcasted_iota(jnp.int32, (STRIP, n), 1)
     sub = lax.broadcasted_iota(jnp.int32, (STRIP, n), 0)
     wide = lax.broadcasted_iota(jnp.int32, (n, n), 1)
-    for start in range(0, n, PANEL):
-        stop = start + PANEL
-        here = (wide >= start) & (wide < stop)
+    pair = wide < 2 * PANEL
+    even = wide % (2 * PANEL) < PANEL
+
+    def body(step, carry):
+        start = pl.multiple_of(step * PANEL, PANEL)
+        here = (wide >= start) & (wide < start + PANEL)
         for mat in mats:
-            strips = [tuple(r[a : a + STRIP, :] for r in mat) for a in range(start, stop, STRIP)]
+            panel = tuple(r[pl.ds(start, PANEL), :] for r in mat)
+            strips = [tuple(v[a : a + STRIP, :] for v in panel) for a in range(0, PANEL, STRIP)]
+            moved = [
+                pltpu.roll(mat[turn % 2][...], n - start + turn * PANEL, 1) for turn in range(4)
+            ]
+            left = jnp.where(
+                pair, jnp.where(even, moved[0], moved[1]), jnp.where(even, moved[2], moved[3])
+            )
+            high, middle, low = thirds(left)
+            left = jnp.concatenate(
+                [high, jnp.where(pair, high, middle), jnp.where(pair, middle, low)], axis=1
+            )
             strips = swept(strips, start, sub, lane)
             panel = [jnp.concatenate([x[c] for x in strips], axis=0) for c in (0, 1)]
-            left = jnp.concatenate([r[:, start:stop] for r in mat], axis=1)
-            change = halves(dot(left, square(panel)))
+            high, middle, low = thirds(square(panel))
+            right = jnp.concatenate([high, middle, low, high, middle, high], axis=0)
+            change = halves(jnp.dot(left, right, preferred_element_type=F32))
             for c in (0, 1):
                 mat[c][...] = jnp.where(here, 0.0, mat[c][...]) - change[c]
-                mat[c][start:stop, :] = panel[c]
+                mat[c][pl.ds(start, PANEL), :] = panel[c]
+        return carry
+
+    lax.fori_loop(0, n // PANEL, body, 0)
 
 
 def packed(x, row, col):
@@ -146,7 +172,7 @@
 def kernel(
     count, onsite_ref, mixing_ref, strength_ref, hopping_ref, energy_ref, broadening_ref,
     real_ref, imag_ref,
-    own_ref, low_ref, high_ref, work, spare,
+    own_ref, low_ref, high_ref, work, spare, weight_low, weight_high,
     packed_out, packed_low, packed_high, link_low, link_high, from_low, from_high, strength_low,
     pack_up_send, pack_up_recv, pack_down_send, pack_down_recv,
     link_up_send, link_up_recv, link_down_send, link_down_recv, raw_send, raw_recv,
@@ -207,6 +233,20 @@
         refs[0][...] = real
         refs[1][...] = broadening
 
+    def keep(ref, wide_value, sign=None):
+        for c, value in enumerate(halves(wide_value)):
+            ref[c] = value if sign is None else sign * value
+
+    def add(ref, wide_value):
+        for c, value in enumerate(halves(wide_value)):
+            ref[c] += value
+
+    def stacked(wide_value):
+        return jnp.concatenate(halves(wide_value), axis=0)
+
+    def side_by_side(tall_value):
+        return jnp.concatenate([tall_value[:n], tall_value[n:]], axis=1)
+
     first = (work.at[0], work.at[1])
     second = (spare.at[0], spare.at[1])
 
@@ -254,14 +294,11 @@
 
     near = coupling(strength_ref, hopping_ref, 0)
     far = jnp.where(me < count - 1, coupling(strength_ref, hopping_ref, 1), 0.0)
-    weight = halves(dot(near, beside(unpacked(packed_out.at[0], row, col))))
-    both = jnp.concatenate([weight[0], weight[1]], axis=0)
-    result = dot(both, near, transpose_b=True)
-    high_ref[0] = result[:n]
-    high_ref[1] = result[n:]
-    result = dot(both, far)
-    link_high[1, 0] = -result[:n]
-    link_high[1, 1] = -result[n:]
+    weight = dot(near, beside(unpacked(packed_out.at[0], row, col)))
+    keep(weight_high, weight, -1.0)
+    keep(high_ref, side_by_side(dot(stacked(weight), near, transpose_b=True)))
+    from_high[0, 0] = -far
+    from_high[0, 1] = jnp.zeros((n, n), F32)
 
     @pl.when(me >= 1)
     def _():
@@ -271,26 +308,17 @@
 
     near = coupling(strength_low, from_low.at[0], 0)
     far = coupling(strength_low, from_low.at[0], 1)
-    weight = halves(dot(far.T, beside(unpacked(packed_low.at[0], row, col))))
-    both = jnp.concatenate([weight[0], weight[1]], axis=0)
-    result = dot(both, far)
-    low_ref[0] = result[:n]
-    low_ref[1] = result[n:]
-    result = dot(both, near, transpose_b=True)
-    link_low[1, 0] = -result[:n]
-    link_low[1, 1] = -result[n:]
+    weight = dot(far.T, beside(unpacked(packed_low.at[0], row, col)))
+    keep(weight_low, weight, -1.0)
+    keep(low_ref, side_by_side(dot(stacked(weight), far)))
+    from_low[0, 0] = -near.T
+    from_low[0, 1] = jnp.zeros((n, n), F32)
 
     def level_step(level, stride):
         has_low = me >= stride
         has_high = me + stride < count
-
-        @pl.when(jnp.logical_and(level < levels, has_high))
-        def _():
-            link_up(level, me + stride).start()
-
-        @pl.when(jnp.logical_and(level < levels, has_low))
-        def _():
-            link_down(level, me - stride).start()
+        inner = jnp.logical_and(has_low, has_high)
+        before = level - 1
 
         first[0][...] = own_ref[...] - low_ref[0] - high_ref[0]
         first[1][...] = broadening - low_ref[1] - high_ref[1]
@@ -305,15 +333,35 @@
         def _():
             pack_down(level, me - stride).start()
 
+        @pl.when(jnp.logical_and(level > 1, has_low))
+        def _():
+            link_up(before, me - stride // 2).wait_recv()
+
+        @pl.when(jnp.logical_and(level > 1, has_high))
+        def _():
+            link_down(before, me + stride // 2).wait_recv()
+
         @pl.when(jnp.logical_not(has_low))
         def _():
-            from_low[level] = jnp.zeros((2, n, n), F32)
+            from_low[before] = jnp.zeros((2, n, n), F32)
             packed_low[level] = jnp.zeros((n + STRIP, n), F32)
 
         @pl.when(jnp.logical_not(has_high))
         def _():
-            from_high[level] = jnp.zeros((2, n, n), F32)
+            from_high[before] = jnp.zeros((2, n, n), F32)
             packed_high[level] = jnp.zeros((n + STRIP, n), F32)
+
+        low = (from_low[before, 0], from_low[before, 1])
+        low = dot(beside((weight_low[0], weight_low[1])), square(low))
+        keep(link_low.at[level], low, -1.0)
+        high = (from_high[before, 0], from_high[before, 1])
+        high = dot(beside((weight_high[0], weight_high[1])), square(high))
+        keep(link_high.at[level], high, -1.0)
+
+        @pl.when(inner)
+        def _():
+            link_up(level, me + stride).start()
+            link_down(level, me - stride).start()
 
         @pl.when(has_low)
         def _():
@@ -325,32 +373,12 @@
 
         low = (link_low[level, 0], link_low[level, 1])
         high = (link_high[level, 0], link_high[level, 1])
-        low_weight = cdot(low, unpacked(packed_low.at[level], row, col))
-        high_weight = cdot(high, unpacked(packed_high.at[level], row, col))
-        term = cdot_t(low_weight, low)
-        low_ref[0] += term[0]
-        low_ref[1] += term[1]
-        term = cdot_t(high_weight, high)
-        high_ref[0] += term[0]
-        high_ref[1] += term[1]
-
-        @pl.when(level < levels)
-        def _():
-            @pl.when(has_low)
-            def _():
-                link_up(level, me - stride).wait_recv()
-
-            @pl.when(has_high)
-            def _():
-                link_down(level, me + stride).wait_recv()
-
-            term = cdot(low_weight, (from_low[level, 0], from_low[level, 1]))
-            link_low[level + 1, 0] = -term[0]
-            link_low[level + 1, 1] = -term[1]
-            term = cdot(high_weight, (from_high[level, 0], from_high[level, 1]))
-            link_high[level + 1, 0] = -term[0]
-            link_high[level + 1, 1] = -term[1]
-
+        low_weight = dot(beside(low), square(unpacked(packed_low.at[level], row, col)))
+        high_weight = dot(beside(high), square(unpacked(packed_high.at[level], row, col)))
+        keep(weight_low, low_weight)
+        keep(weight_high, high_weight)
+        add(low_ref, dot(low_weight, square_t(low), transpose_b=True))
+        add(high_ref, dot(high_weight, square_t(high), transpose_b=True))
         return stride * 2
 
     lax.fori_loop(1, levels + 1, level_step, 1)
@@ -416,12 +444,9 @@
         def _():
             pack_down(level, me - stride).wait_send()
 
-        @pl.when(jnp.logical_and(level < levels, has_high))
+        @pl.when(jnp.logical_and(has_low, has_high))
         def _():
             link_up(level, me + stride).wait_send()
-
-        @pl.when(jnp.logical_and(level < levels, has_low))
-        def _():
             link_down(level, me - stride).wait_send()
 
         return stride * 2
@@ -452,6 +477,8 @@
                 pltpu.VMEM((2, n, n), F32),
                 pltpu.VMEM((2, n, n), F32),
                 pltpu.VMEM((2, n, n), F32),
+                pltpu.VMEM((2, n, n), F32),
+                pltpu.VMEM((2, n, n), F32),
                 pack_shape, pack_shape, pack_shape,
                 link_shape, link_shape, link_shape, link_shape,
                 pltpu.VMEM((2, n), F32),

time: 150 us -> 130 us (0.87); the launches traced: 147 us -> 130 us
  Pallas kernels: 142 us -> 125 us
    pallas_call x1, Pallas kernels: 142 us -> 125 us  [shards(): pl.pallas_call(functools.partial(kernel, count), out_shape=(pair, pair),...]
where the time goes in v2:
time: 130 us
  Pallas kernels  125 us (96%)
  local copies, waits for them, and re-layouts  3.12 us (2%)
  between operations  2 us (2%)
    pallas_call x1, Pallas kernels, shards(): pl.pallas_call(functools.partial(kernel, count), out_shape=(pair, pair),...  125 us
    unnamed x10, local copies, waits for them, and re-layouts  3.12 us

profile of v2, /device:TPU:34, one launch (start us, length us, event | category | flops | bytes accessed | tf_op | source)
XLA Modules:
  0.0 130.2 jit_solution(7176345377694756087)
XLA Ops:
  0.6 0.0 copy-start.3
  1.3 0.0 copy-start.2
  2.0 0.0 copy-done.3
  2.0 0.0 copy-done.2
  2.0 0.0 copy-start
  2.0 0.9 copy-done
  2.9 0.0 copy-start.1
  2.9 0.9 copy-done.1
  3.8 125.0 %shard_map.77 = (f32[2,128,128]{2,1,0:T(8,128)S(1)}, f32[2,128,128]{2,1,0:T(8,128)S(1)}) custom-call(f32[2,128]{1,0:T(2,128)S(1)} %copy-done.2, f32[2,128,128]{2,1,0:T(8,128)S(1)} %copy-done, f32[2,128]{1,0:T(2,128)S(1)} %copy-done.3, f32[2,128,128]{2,1,0:T(8,128)S(1)} %copy-done.1, f32[1]{0:T(128)S(6)} %copy.10.energy_ref, f32[1]{0:T(128)S(6)} %copy.11.broadening_ref), custom_call_target="tpu_custom_call" | custom-call | tf_op jit(solution)/shard_map/pallas_call | solution.py:469
  128.9 0.7 copy.12
  129.5 0.7 copy.13
Async XLA Ops:
  0.6 1.3 %copy-start.3 = (f32[2,128]{1,0:T(2,128)S(1)}, f32[2,128]{1,0:T(2,128)}, u32[]{:S(2)}) copy-start(f32[2,128]{1,0:T(2,128)} %strength_ref.1) | copy-start | bytes 3076
  1.3 0.7 copy-start.2
  2.0 0.9 copy-start
  2.9 0.9 copy-start.1

commit v3 on v2

--- a/solution.py
+++ b/solution.py
@@ -17,6 +17,10 @@
     return a[0] * b[0] - a[1] * b[1], a[0] * b[1] + a[1] * b[0]
 
 
+def plus(a, b):
+    return a[0] + b[0], a[1] + b[1]
+
+
 def minus(a, b):
     return a[0] - b[0], a[1] - b[1]
 
@@ -68,25 +72,33 @@
 
 def eliminated(rows, columns, first, sub, lane):
     zero = jnp.zeros_like(rows[0])
+    none = (zero, zero)
     eye = jnp.where(lane - first == sub, 1.0, 0.0)
     rows = select((lane >= first) & (lane < first + STRIP), (eye, zero), rows)
-    for j in range(STRIP):
-        own = sub == j
-        factor = columns[j]
-        pivot = row_of(factor, j)
-        scale = 1.0 / (pivot[0] * pivot[0] + pivot[1] * pivot[1])
-        inverse = (pivot[0] * scale, -pivot[1] * scale)
-        if j + 1 < STRIP:
-            entry = row_of(columns[j + 1], j)
-            change = select(own, (-entry[0], -entry[1]), times(factor, entry))
-            columns[j + 1] = minus(
-                select(own, (zero, zero), columns[j + 1]), times(change, inverse)
-            )
-        factor = select(own, (-inverse[0], -inverse[1]), times(factor, inverse))
-        for k in range(j + 2, STRIP):
-            change = times(factor, row_of(columns[k], j))
-            columns[k] = minus(select(own, (zero, zero), columns[k]), change)
-        rows = minus(select(own, (zero, zero), rows), times(factor, row_of(rows, j)))
+    for j in range(0, STRIP, 2):
+        top, bottom = sub == j, sub == j + 1
+        own = top | bottom
+        f, g = columns[j], columns[j + 1]
+        a, c = row_of(f, j), row_of(f, j + 1)
+        b, d = row_of(g, j), row_of(g, j + 1)
+        det = minus(times(a, d), times(b, c))
+        scale = 1.0 / (det[0] * det[0] + det[1] * det[1])
+        inverse = (det[0] * scale, -det[1] * scale)
+        u = minus(times(f, d), times(g, c))
+        v = minus(times(g, a), times(f, b))
+        u = select(top, (-d[0], -d[1]), select(bottom, c, u))
+        v = select(top, b, select(bottom, (-a[0], -a[1]), v))
+
+        def change(x, u, v):
+            return plus(times(u, row_of(x, j)), times(v, row_of(x, j + 1)))
+
+        for k in range(j + 2, min(j + 4, STRIP)):
+            x = columns[k]
+            columns[k] = minus(select(own, none, x), times(change(x, u, v), inverse))
+        u, v = times(u, inverse), times(v, inverse)
+        for k in range(j + 4, STRIP):
+            columns[k] = minus(select(own, none, columns[k]), change(columns[k], u, v))
+        rows = minus(select(own, none, rows), change(rows, u, v))
     return rows
 
 
@@ -363,6 +375,12 @@
             link_up(level, me + stride).start()
             link_down(level, me - stride).start()
 
+        @pl.when(level == levels)
+        def _():
+            second[0][...] = own_ref[...] - jnp.where(has_low, high_ref[0], low_ref[0])
+            second[1][...] = broadening - jnp.where(has_low, high_ref[1], low_ref[1])
+            invert((second,))
+
         @pl.when(has_low)
         def _():
             pack_up(level, me - stride).wait_recv()
@@ -383,12 +401,14 @@
 
     lax.fori_loop(1, levels + 1, level_step, 1)
 
-    first[0][...] = own_ref[...] - high_ref[0]
-    first[1][...] = broadening - high_ref[1]
-    second[0][...] = own_ref[...] - low_ref[0]
-    second[1][...] = broadening - low_ref[1]
-    invert((first, second))
-    pack(last, (first[0][...], first[1][...]))
+    upper = me >= count // 2
+    first[0][...] = own_ref[...] - jnp.where(upper, low_ref[0], high_ref[0])
+    first[1][...] = broadening - jnp.where(upper, low_ref[1], high_ref[1])
+    invert((first,))
+    pack(last, [jnp.where(upper, spare[c], work[c]) for c in (0, 1)])
+    left = [jnp.where(upper, work[c], spare[c]) for c in (0, 1)]
+    left = [0.5 * (value + value.T) for value in left]
+    keep(weight_low, beside(left))
 
     @pl.when(me >= 1)
     def _():
@@ -406,8 +426,7 @@
 
     near = coupling(strength_ref, hopping_ref, 0)
     far = jnp.where(me < count - 1, coupling(strength_ref, hopping_ref, 1), 0.0)
-    mean = [0.5 * (ref[...] + ref[...].T) for ref in second]
-    weight = halves(dot(near.T, beside(mean)))
+    weight = halves(dot(near.T, beside((weight_low[0], weight_low[1]))))
     below = dot(jnp.concatenate([weight[0], weight[1]], axis=0), near)
 
     @pl.when(me + 1 < count)

time: 130 us -> 123 us (0.946)
  Pallas kernels: 125 us -> 118 us
    pallas_call x1, Pallas kernels: 125 us -> 118 us  [shards(): pl.pallas_call(functools.partial(kernel, count), out_shape=(pair, pair),...]
where the time goes in v3:
time: 123 us
  Pallas kernels  118 us (96%)
  local copies, waits for them, and re-layouts  3.12 us (3%)
  between operations  2 us (2%)
    pallas_call x1, Pallas kernels, shards(): pl.pallas_call(functools.partial(kernel, count), out_shape=(pair, pair),...  118 us
    unnamed x10, local copies, waits for them, and re-layouts  3.12 us

profile of v3, /device:TPU:34, one launch (start us, length us, event | category | flops | bytes accessed | tf_op | source)
XLA Modules:
  0.0 122.8 jit_solution(888466760907153554)
XLA Ops:
  0.6 0.0 copy-start.3
  1.3 0.0 copy-start.2
  2.0 0.0 copy-done.3
  2.0 0.0 copy-done.2
  2.0 0.0 copy-start
  2.0 0.9 copy-done
  2.9 0.0 copy-start.1
  2.9 0.9 copy-done.1
  3.8 117.7 %shard_map.77 = (f32[2,128,128]{2,1,0:T(8,128)S(1)}, f32[2,128,128]{2,1,0:T(8,128)S(1)}) custom-call(f32[2,128]{1,0:T(2,128)S(1)} %copy-done.2, f32[2,128,128]{2,1,0:T(8,128)S(1)} %copy-done, f32[2,128]{1,0:T(2,128)S(1)} %copy-done.3, f32[2,128,128]{2,1,0:T(8,128)S(1)} %copy-done.1, f32[1]{0:T(128)S(6)} %copy.10.energy_ref, f32[1]{0:T(128)S(6)} %copy.11.broadening_ref), custom_call_target="tpu_custom_call" | custom-call | tf_op jit(solution)/shard_map/pallas_call | solution.py:488
  121.5 0.7 copy.12
  122.1 0.7 copy.13
Async XLA Ops:
  0.6 1.3 %copy-start.3 = (f32[2,128]{1,0:T(2,128)S(1)}, f32[2,128]{1,0:T(2,128)}, u32[]{:S(2)}) copy-start(f32[2,128]{1,0:T(2,128)} %strength_ref.1) | copy-start | bytes 3076
  1.3 0.7 copy-start.2
  2.0 0.9 copy-start
  2.9 0.9 copy-start.1

commit v4 on v3

--- a/solution.py
+++ b/solution.py
@@ -182,13 +182,28 @@
 
 
 def kernel(
-    count, onsite_ref, mixing_ref, strength_ref, hopping_ref, energy_ref, broadening_ref,
+    count, onsite_hbm, mixing_hbm, strength_hbm, hopping_hbm, energy_ref, broadening_ref,
     real_ref, imag_ref,
+    onsite_ref, mixing_ref, strength_ref, hopping_ref, input_sem,
     own_ref, low_ref, high_ref, work, spare, weight_low, weight_high,
-    packed_out, packed_low, packed_high, link_low, link_high, from_low, from_high, strength_low,
+    packed_out, packed_low, packed_high, link_low, link_high, from_low, from_high,
     pack_up_send, pack_up_recv, pack_down_send, pack_down_recv,
-    link_up_send, link_up_recv, link_down_send, link_down_recv, raw_send, raw_recv,
+    link_up_send, link_up_recv, link_down_send, link_down_recv,
 ):
+    pieces = [
+        pltpu.make_async_copy(source, target, input_sem.at[i])
+        for i, (source, target) in enumerate(
+            (
+                (onsite_hbm, onsite_ref),
+                (mixing_hbm, mixing_ref),
+                (strength_hbm, strength_ref),
+                (hopping_hbm, hopping_ref),
+            )
+        )
+    ]
+    for piece in pieces:
+        piece.start()
+
     levels = count.bit_length() - 1
     last = levels + 1
     n = mixing_ref.shape[1]
@@ -230,21 +245,11 @@
         return copy(link_high.at[slot], from_high.at[slot], link_down_send.at[slot],
                     link_down_recv.at[slot], slab)
 
-    def raw_mixing(slab):
-        return copy(hopping_ref, from_low.at[0], raw_send.at[0], raw_recv.at[0], slab)
-
-    def raw_strength(slab):
-        return copy(strength_ref, strength_low, raw_send.at[1], raw_recv.at[1], slab)
-
     def pack(slot, value):
         square_part, tail_part = packed(value, row, col)
         packed_out[slot, 0:n, :] = square_part
         packed_out[slot, n : n + STRIP, :] = tail_part
 
-    def set_work(refs, real):
-        refs[0][...] = real
-        refs[1][...] = broadening
-
     def keep(ref, wide_value, sign=None):
         for c, value in enumerate(halves(wide_value)):
             ref[c] = value if sign is None else sign * value
@@ -278,6 +283,18 @@
                 barrier, inc=1, device_id={"slab": me + stride}, device_id_type=MESH
             )
 
+    for piece in pieces:
+        piece.wait()
+    mine = coupling(strength_ref, hopping_ref, 0)
+    next_one = jnp.where(me < count - 1, coupling(strength_ref, hopping_ref, 1), 0.0)
+
+    own_ref[...] = onsite(0)
+    first[0][...] = onsite(1)
+    first[1][...] = broadening
+    invert((first,))
+    inverse = beside([0.5 * (ref[...] + ref[...].T) for ref in first])
+    weight = dot(next_one.T, inverse)
+    pack(0, halves(side_by_side(dot(stacked(weight), next_one))))
     peers = 0
     for level in range(levels):
         stride = 1 << level
@@ -286,45 +303,28 @@
 
     @pl.when(me + 1 < count)
     def _():
-        raw_mixing(me + 1).start()
-        raw_strength(me + 1).start()
+        pack_up(0, me + 1).start()
+
+    keep(link_low.at[0], side_by_side(dot(stacked(weight), mine, transpose_b=True)), -1.0)
+
+    @pl.when(me + 1 < count)
+    def _():
+        link_up(0, me + 1).start()
 
     @pl.when(me < 1)
     def _():
         from_low[0] = jnp.zeros((2, n, n), F32)
-        strength_low[...] = jnp.zeros((2, n), F32)
         packed_low[0] = jnp.zeros((n + STRIP, n), F32)
 
-    own_ref[...] = onsite(0)
-    set_work(first, onsite(1))
-    invert((first,))
-    pack(0, (first[0][...], first[1][...]))
-
-    @pl.when(me + 1 < count)
-    def _():
-        pack_up(0, me + 1).start()
-
-    near = coupling(strength_ref, hopping_ref, 0)
-    far = jnp.where(me < count - 1, coupling(strength_ref, hopping_ref, 1), 0.0)
-    weight = dot(near, beside(unpacked(packed_out.at[0], row, col)))
-    keep(weight_high, weight, -1.0)
-    keep(high_ref, side_by_side(dot(stacked(weight), near, transpose_b=True)))
-    from_high[0, 0] = -far
-    from_high[0, 1] = jnp.zeros((n, n), F32)
+    weight = dot(mine, inverse)
+    keep(high_ref, side_by_side(dot(stacked(weight), mine, transpose_b=True)))
+    keep(link_high.at[1], side_by_side(dot(stacked(weight), next_one)), -1.0)
 
     @pl.when(me >= 1)
     def _():
-        raw_mixing(me).wait_recv()
-        raw_strength(me).wait_recv()
-        pack_up(0, me).wait_recv()
-
-    near = coupling(strength_low, from_low.at[0], 0)
-    far = coupling(strength_low, from_low.at[0], 1)
-    weight = dot(far.T, beside(unpacked(packed_low.at[0], row, col)))
-    keep(weight_low, weight, -1.0)
-    keep(low_ref, side_by_side(dot(stacked(weight), far)))
-    from_low[0, 0] = -near.T
-    from_low[0, 1] = jnp.zeros((n, n), F32)
+        pack_up(0, me - 1).wait_recv()
+
+    keep(low_ref, beside(unpacked(packed_low.at[0], row, col)))
 
     def level_step(level, stride):
         has_low = me >= stride
@@ -345,30 +345,46 @@
         def _():
             pack_down(level, me - stride).start()
 
-        @pl.when(jnp.logical_and(level > 1, has_low))
-        def _():
-            link_up(before, me - stride // 2).wait_recv()
-
-        @pl.when(jnp.logical_and(level > 1, has_high))
-        def _():
-            link_down(before, me + stride // 2).wait_recv()
-
         @pl.when(jnp.logical_not(has_low))
         def _():
-            from_low[before] = jnp.zeros((2, n, n), F32)
             packed_low[level] = jnp.zeros((n + STRIP, n), F32)
 
         @pl.when(jnp.logical_not(has_high))
         def _():
-            from_high[before] = jnp.zeros((2, n, n), F32)
             packed_high[level] = jnp.zeros((n + STRIP, n), F32)
 
-        low = (from_low[before, 0], from_low[before, 1])
-        low = dot(beside((weight_low[0], weight_low[1])), square(low))
-        keep(link_low.at[level], low, -1.0)
-        high = (from_high[before, 0], from_high[before, 1])
-        high = dot(beside((weight_high[0], weight_high[1])), square(high))
-        keep(link_high.at[level], high, -1.0)
+        @pl.when(level == 1)
+        def _():
+            @pl.when(has_low)
+            def _():
+                link_up(0, me - 1).wait_recv()
+
+            link_low[1] = from_low[0]
+
+        @pl.when(level > 1)
+        def _():
+            @pl.when(has_low)
+            def _():
+                link_up(before, me - stride // 2).wait_recv()
+
+            @pl.when(has_high)
+            def _():
+                link_down(before, me + stride // 2).wait_recv()
+
+            @pl.when(jnp.logical_not(has_low))
+            def _():
+                from_low[before] = jnp.zeros((2, n, n), F32)
+
+            @pl.when(jnp.logical_not(has_high))
+            def _():
+                from_high[before] = jnp.zeros((2, n, n), F32)
+
+            low = (from_low[before, 0], from_low[before, 1])
+            low = dot(beside((weight_low[0], weight_low[1])), square(low))
+            keep(link_low.at[level], low, -1.0)
+            high = (from_high[before, 0], from_high[before, 1])
+            high = dot(beside((weight_high[0], weight_high[1])), square(high))
+            keep(link_high.at[level], high, -1.0)
 
         @pl.when(inner)
         def _():
@@ -424,17 +440,15 @@
     real_ref[0] = first[0][...]
     imag_ref[0] = first[1][...]
 
-    near = coupling(strength_ref, hopping_ref, 0)
-    far = jnp.where(me < count - 1, coupling(strength_ref, hopping_ref, 1), 0.0)
-    weight = halves(dot(near.T, beside((weight_low[0], weight_low[1]))))
-    below = dot(jnp.concatenate([weight[0], weight[1]], axis=0), near)
+    weight = halves(dot(mine.T, beside((weight_low[0], weight_low[1]))))
+    below = dot(jnp.concatenate([weight[0], weight[1]], axis=0), mine)
 
     @pl.when(me + 1 < count)
     def _():
         pack_down(last, me + 1).wait_recv()
 
-    weight = halves(dot(far, beside(unpacked(packed_high.at[last], row, col))))
-    above = dot(jnp.concatenate([weight[0], weight[1]], axis=0), far, transpose_b=True)
+    weight = halves(dot(next_one, beside(unpacked(packed_high.at[last], row, col))))
+    above = dot(jnp.concatenate([weight[0], weight[1]], axis=0), next_one, transpose_b=True)
     first[0][...] = onsite(1) - below[:n] - above[:n]
     first[1][...] = broadening - below[n:] - above[n:]
     invert((first,))
@@ -443,9 +457,8 @@
 
     @pl.when(me + 1 < count)
     def _():
-        raw_mixing(me + 1).wait_send()
-        raw_strength(me + 1).wait_send()
         pack_up(0, me + 1).wait_send()
+        link_up(0, me + 1).wait_send()
 
     @pl.when(me >= 1)
     def _():
@@ -488,9 +501,14 @@
         return pl.pallas_call(
             functools.partial(kernel, count),
             out_shape=(pair, pair),
-            in_specs=[whole] * 4 + [scalar] * 2,
+            in_specs=[pl.BlockSpec(memory_space=pltpu.HBM)] * 4 + [scalar] * 2,
             out_specs=(whole, whole),
             scratch_shapes=[
+                pltpu.VMEM((2, n), F32),
+                pltpu.VMEM((2, n, n), F32),
+                pltpu.VMEM((2, n), F32),
+                pltpu.VMEM((2, n, n), F32),
+                pltpu.SemaphoreType.DMA((4,)),
                 pltpu.VMEM((n, n), F32),
                 pltpu.VMEM((2, n, n), F32),
                 pltpu.VMEM((2, n, n), F32),
@@ -500,10 +518,8 @@
                 pltpu.VMEM((2, n, n), F32),
                 pack_shape, pack_shape, pack_shape,
                 link_shape, link_shape, link_shape, link_shape,
-                pltpu.VMEM((2, n), F32),
             ]
-            + [sems] * 8
-            + [pltpu.SemaphoreType.DMA((2,))] * 2,
+            + [sems] * 8,
             compiler_params=pltpu.CompilerParams(
                 collective_id=0, has_side_effects=True, vmem_limit_bytes=40 * 1024 * 1024
             ),

time: 123 us -> 121 us (0.984)
  Pallas kernels: 118 us -> 116 us
    pallas_call x1, Pallas kernels: 118 us -> 116 us  [shards(): pl.pallas_call(functools.partial(kernel, count), out_shape=(pair, pair),...]
where the time goes in v4:
time: 121 us
  Pallas kernels  116 us (96%)
  local copies, waits for them, and re-layouts  3.12 us (3%)
  between operations  2 us (2%)
    pallas_call x1, Pallas kernels, shards(): pl.pallas_call(functools.partial(kernel, count), out_shape=(pair, pair),...  116 us
    unnamed x10, local copies, waits for them, and re-layouts  3.12 us

profile of v4, /device:TPU:34, one launch (start us, length us, event | category | flops | bytes accessed | tf_op | source)
XLA Modules:
  0.0 120.8 jit_solution(10925867377152406464)
XLA Ops:
  0.6 0.0 copy-start.3
  1.3 0.0 copy-start.2
  2.0 0.0 copy-done.3
  2.0 0.0 copy-done.2
  2.0 0.0 copy-start
  2.0 0.9 copy-done
  2.9 0.0 copy-start.1
  2.9 0.9 copy-done.1
  3.8 115.7 %shard_map.77 = (f32[2,128,128]{2,1,0:T(8,128)S(1)}, f32[2,128,128]{2,1,0:T(8,128)S(1)}) custom-call(f32[2,128]{1,0:T(2,128)S(1)} %copy-done.2, f32[2,128,128]{2,1,0:T(8,128)S(1)} %copy-done, f32[2,128]{1,0:T(2,128)S(1)} %copy-done.3, f32[2,128,128]{2,1,0:T(8,128)S(1)} %copy-done.1, f32[1]{0:T(128)S(6)} %copy.10.energy_ref, f32[1]{0:T(128)S(6)} %copy.11.broadening_ref), custom_call_target="tpu_custom_call" | custom-call | tf_op jit(solution)/shard_map/pallas_call | solution.py:501
  119.5 0.7 copy.12
  120.1 0.7 copy.13
Async XLA Ops:
  0.6 1.3 %copy-start.3 = (f32[2,128]{1,0:T(2,128)S(1)}, f32[2,128]{1,0:T(2,128)}, u32[]{:S(2)}) copy-start(f32[2,128]{1,0:T(2,128)} %strength_hbm.1) | copy-start | bytes 3076
  1.3 0.7 copy-start.2
  2.0 0.9 copy-start
  2.9 0.9 copy-start.1

commit v5 on v4

--- a/solution.py
+++ b/solution.py
@@ -128,7 +128,7 @@
     return high, middle, (rest - middle.astype(F32)).astype(jnp.bfloat16)
 
 
-def invert(mats):
+def invert(mats, low_panel=0, high_panel=None):
     n = mats[0][0].shape[0]
     lane = lax.broadcasted_iota(jnp.int32, (STRIP, n), 1)
     sub = lax.broadcasted_iota(jnp.int32, (STRIP, n), 0)
@@ -162,7 +162,7 @@
                 mat[c][pl.ds(start, PANEL), :] = panel[c]
         return carry
 
-    lax.fori_loop(0, n // PANEL, body, 0)
+    lax.fori_loop(low_panel, high_panel or n // PANEL, body, 0)
 
 
 def packed(x, row, col):
@@ -187,8 +187,11 @@
     onsite_ref, mixing_ref, strength_ref, hopping_ref, input_sem,
     own_ref, low_ref, high_ref, work, spare, weight_low, weight_high,
     packed_out, packed_low, packed_high, link_low, link_high, from_low, from_high,
+    half_out, half_low, half_high, rest_out, rest_low, rest_high,
     pack_up_send, pack_up_recv, pack_down_send, pack_down_recv,
     link_up_send, link_up_recv, link_down_send, link_down_recv,
+    half_up_send, half_up_recv, half_down_send, half_down_recv,
+    rest_up_send, rest_up_recv, rest_down_send, rest_down_recv,
 ):
     pieces = [
         pltpu.make_async_copy(source, target, input_sem.at[i])
@@ -245,6 +248,22 @@
         return copy(link_high.at[slot], from_high.at[slot], link_down_send.at[slot],
                     link_down_recv.at[slot], slab)
 
+    def half_up(slot, slab):
+        return copy(half_out.at[slot], half_low.at[slot], half_up_send.at[slot],
+                    half_up_recv.at[slot], slab)
+
+    def half_down(slot, slab):
+        return copy(half_out.at[slot], half_high.at[slot], half_down_send.at[slot],
+                    half_down_recv.at[slot], slab)
+
+    def rest_up(slot, slab):
+        return copy(rest_out.at[slot], rest_low.at[slot], rest_up_send.at[slot],
+                    rest_up_recv.at[slot], slab)
+
+    def rest_down(slot, slab):
+        return copy(rest_out.at[slot], rest_high.at[slot], rest_down_send.at[slot],
+                    rest_down_recv.at[slot], slab)
+
     def pack(slot, value):
         square_part, tail_part = packed(value, row, col)
         packed_out[slot, 0:n, :] = square_part
@@ -263,6 +282,40 @@
 
     def side_by_side(tall_value):
         return jnp.concatenate([tall_value[:n], tall_value[n:]], axis=1)
+
+    m = n // 2
+    left_lanes = col < m
+
+    def mixed(link, half_ref):
+        block = (half_ref[0], half_ref[1])
+        lhs = jnp.where(left_lanes, link[0], pltpu.roll(link[1], m, 1))
+        product = halves(dot(lhs, square(block)))
+        ahead = [
+            jnp.where(left_lanes, value, both - value) for value, both in zip(product, link)
+        ]
+        other = [jnp.where(left_lanes, both, value) for value, both in zip(ahead, link)]
+        return ahead, other
+
+    def finished(ahead, rest_ref):
+        lhs = jnp.where(left_lanes, pltpu.roll(ahead[0], m, 1), ahead[1])
+        rest = rest_ref[...]
+        turned = pltpu.roll(rest, m, 1)
+        turned = jnp.where(left_lanes[:m], -turned, turned)
+        product = dot(lhs, jnp.concatenate([rest, turned], axis=0))
+        return (
+            jnp.where(left_lanes, ahead[0], pltpu.roll(product, m, 1)),
+            jnp.where(left_lanes, ahead[1], product),
+        )
+
+    def reduced(link, half_ref):
+        turned = [half_ref[c].T[m:, :] for c in (0, 1)]
+        change = dot(
+            jnp.concatenate(turned, axis=1), square((link[0][:m], link[1][:m]))
+        )
+        return [
+            jnp.concatenate([link[c][:m], link[c][m:] - part], axis=0)
+            for c, part in enumerate(halves(change))
+        ]
 
     first = (work.at[0], work.at[1])
     second = (spare.at[0], spare.at[1])
@@ -334,24 +387,41 @@
 
         first[0][...] = own_ref[...] - low_ref[0] - high_ref[0]
         first[1][...] = broadening - low_ref[1] - high_ref[1]
-        invert((first,))
-        pack(level, (first[0][...], first[1][...]))
+        invert((first,), 0, n // PANEL // 2)
+        for c in (0, 1):
+            turned = first[c][...].T[:m]
+            turned = jnp.where(left_lanes[:m], turned, -turned)
+            half_out[level, c] = 0.5 * (first[c][0:m, :] + turned)
 
         @pl.when(has_high)
         def _():
-            pack_up(level, me + stride).start()
+            half_up(level, me + stride).start()
 
         @pl.when(has_low)
         def _():
-            pack_down(level, me - stride).start()
+            half_down(level, me - stride).start()
+
+        invert((first,), n // PANEL // 2, n // PANEL)
+        mean = [0.5 * (ref[m:, :] + ref[...].T[m:]) for ref in first]
+        rest_out[level] = jnp.where(left_lanes[:m], pltpu.roll(mean[0], m, 1), mean[1])
+
+        @pl.when(has_high)
+        def _():
+            rest_up(level, me + stride).start()
+
+        @pl.when(has_low)
+        def _():
+            rest_down(level, me - stride).start()
 
         @pl.when(jnp.logical_not(has_low))
         def _():
-            packed_low[level] = jnp.zeros((n + STRIP, n), F32)
+            half_low[level] = jnp.zeros((2, m, n), F32)
+            rest_low[level] = jnp.zeros((m, n), F32)
 
         @pl.when(jnp.logical_not(has_high))
         def _():
-            packed_high[level] = jnp.zeros((n + STRIP, n), F32)
+            half_high[level] = jnp.zeros((2, m, n), F32)
+            rest_high[level] = jnp.zeros((m, n), F32)
 
         @pl.when(level == 1)
         def _():
@@ -380,16 +450,13 @@
                 from_high[before] = jnp.zeros((2, n, n), F32)
 
             low = (from_low[before, 0], from_low[before, 1])
+            low = reduced(low, half_low.at[before])
             low = dot(beside((weight_low[0], weight_low[1])), square(low))
             keep(link_low.at[level], low, -1.0)
             high = (from_high[before, 0], from_high[before, 1])
+            high = reduced(high, half_high.at[before])
             high = dot(beside((weight_high[0], weight_high[1])), square(high))
             keep(link_high.at[level], high, -1.0)
-
-        @pl.when(inner)
-        def _():
-            link_up(level, me + stride).start()
-            link_down(level, me - stride).start()
 
         @pl.when(level == levels)
         def _():
@@ -399,20 +466,36 @@
 
         @pl.when(has_low)
         def _():
-            pack_up(level, me - stride).wait_recv()
+            half_up(level, me - stride).wait_recv()
 
         @pl.when(has_high)
         def _():
-            pack_down(level, me + stride).wait_recv()
-
-        low = (link_low[level, 0], link_low[level, 1])
-        high = (link_high[level, 0], link_high[level, 1])
-        low_weight = dot(beside(low), square(unpacked(packed_low.at[level], row, col)))
-        high_weight = dot(beside(high), square(unpacked(packed_high.at[level], row, col)))
+            half_down(level, me + stride).wait_recv()
+
+        low, low_other = mixed((link_low[level, 0], link_low[level, 1]), half_low.at[level])
+        high, high_other = mixed((link_high[level, 0], link_high[level, 1]), half_high.at[level])
+        low_other = square_t(low_other)
+        high_other = square_t(high_other)
+
+        @pl.when(has_low)
+        def _():
+            rest_up(level, me - stride).wait_recv()
+
+        @pl.when(has_high)
+        def _():
+            rest_down(level, me + stride).wait_recv()
+
+        @pl.when(inner)
+        def _():
+            link_up(level, me + stride).start()
+            link_down(level, me - stride).start()
+
+        low_weight = beside(finished(low, rest_low.at[level]))
+        high_weight = beside(finished(high, rest_high.at[level]))
+        add(low_ref, dot(low_weight, low_other, transpose_b=True))
+        add(high_ref, dot(high_weight, high_other, transpose_b=True))
         keep(weight_low, low_weight)
         keep(weight_high, high_weight)
-        add(low_ref, dot(low_weight, square_t(low), transpose_b=True))
-        add(high_ref, dot(high_weight, square_t(high), transpose_b=True))
         return stride * 2
 
     lax.fori_loop(1, levels + 1, level_step, 1)
@@ -470,11 +553,13 @@
 
         @pl.when(has_high)
         def _():
-            pack_up(level, me + stride).wait_send()
+            half_up(level, me + stride).wait_send()
+            rest_up(level, me + stride).wait_send()
 
         @pl.when(has_low)
         def _():
-            pack_down(level, me - stride).wait_send()
+            half_down(level, me - stride).wait_send()
+            rest_down(level, me - stride).wait_send()
 
         @pl.when(jnp.logical_and(has_low, has_high))
         def _():
@@ -497,6 +582,8 @@
         pair = jax.ShapeDtypeStruct((2, n, n), F32)
         pack_shape = pltpu.VMEM((levels + 2, n + STRIP, n), F32)
         link_shape = pltpu.VMEM((levels + 1, 2, n, n), F32)
+        half_shape = pltpu.VMEM((levels + 1, 2, n // 2, n), F32)
+        rest_shape = pltpu.VMEM((levels + 1, n // 2, n), F32)
         sems = pltpu.SemaphoreType.DMA((levels + 2,))
         return pl.pallas_call(
             functools.partial(kernel, count),
@@ -518,8 +605,10 @@
                 pltpu.VMEM((2, n, n), F32),
                 pack_shape, pack_shape, pack_shape,
                 link_shape, link_shape, link_shape, link_shape,
+                half_shape, half_shape, half_shape,
+                rest_shape, rest_shape, rest_shape,
             ]
-            + [sems] * 8,
+            + [sems] * 16,
             compiler_params=pltpu.CompilerParams(
                 collective_id=0, has_side_effects=True, vmem_limit_bytes=40 * 1024 * 1024
             ),

time: 121 us -> 125 us (1.033)
  Pallas kernels: 116 us -> 119 us
    pallas_call x1, Pallas kernels: 116 us -> 119 us  [shards(): pl.pallas_call(functools.partial(kernel, count), out_shape=(pair, pair),...]
where the time goes in v5:
time: 125 us; the launch traced here: 124 us
  Pallas kernels  119 us (95%)
  local copies, waits for them, and re-layouts  3.12 us (2%)
  between operations  2 us (2%)
    pallas_call x1, Pallas kernels, shards(): pl.pallas_call(functools.partial(kernel, count), out_shape=(pair, pair),...  119 us
    unnamed x10, local copies, waits for them, and re-layouts  3.12 us

profile of v5, /device:TPU:34, one launch (start us, length us, event | category | flops | bytes accessed | tf_op | source)
XLA Modules:
  0.0 123.7 jit_solution(9150592122274883459)
XLA Ops:
  0.6 0.0 copy-start.3
  1.3 0.0 copy-start.2
  2.0 0.0 copy-done.3
  2.0 0.0 copy-done.2
  2.0 0.0 copy-start
  2.0 0.9 copy-done
  2.9 0.0 copy-start.1
  2.9 0.9 copy-done.1
  3.8 118.6 %shard_map.77 = (f32[2,128,128]{2,1,0:T(8,128)S(1)}, f32[2,128,128]{2,1,0:T(8,128)S(1)}) custom-call(f32[2,128]{1,0:T(2,128)S(1)} %copy-done.2, f32[2,128,128]{2,1,0:T(8,128)S(1)} %copy-done, f32[2,128]{1,0:T(2,128)S(1)} %copy-done.3, f32[2,128,128]{2,1,0:T(8,128)S(1)} %copy-done.1, f32[1]{0:T(128)S(6)} %copy.10.energy_ref, f32[1]{0:T(128)S(6)} %copy.11.broadening_ref), custom_call_target="tpu_custom_call" | custom-call | tf_op jit(solution)/shard_map/pallas_call | solution.py:588
  122.4 0.7 copy.12
  123.1 0.7 copy.13
Async XLA Ops:
  0.6 1.3 %copy-start.3 = (f32[2,128]{1,0:T(2,128)S(1)}, f32[2,128]{1,0:T(2,128)}, u32[]{:S(2)}) copy-start(f32[2,128]{1,0:T(2,128)} %strength_hbm.1) | copy-start | bytes 3076
  1.3 0.7 copy-start.2
  2.0 0.9 copy-start
  2.9 0.9 copy-start.1

commit v6 on v4

--- a/solution.py
+++ b/solution.py
@@ -186,7 +186,7 @@
     real_ref, imag_ref,
     onsite_ref, mixing_ref, strength_ref, hopping_ref, input_sem,
     own_ref, low_ref, high_ref, work, spare, weight_low, weight_high,
-    packed_out, packed_low, packed_high, link_low, link_high, from_low, from_high,
+    packed_out, packed_low, packed_high, link_low, link_high, from_low, from_high, crossed, cross_sem,
     pack_up_send, pack_up_recv, pack_down_send, pack_down_recv,
     link_up_send, link_up_recv, link_down_send, link_down_recv,
 ):
@@ -245,6 +245,9 @@
         return copy(link_high.at[slot], from_high.at[slot], link_down_send.at[slot],
                     link_down_recv.at[slot], slab)
 
+    def cross_down(slot, slab):
+        return copy(link_low.at[slot], crossed, cross_sem.at[0], cross_sem.at[1], slab)
+
     def pack(slot, value):
         square_part, tail_part = packed(value, row, col)
         packed_out[slot, 0:n, :] = square_part
@@ -331,6 +334,9 @@
         has_high = me + stride < count
         inner = jnp.logical_and(has_low, has_high)
         before = level - 1
+        crossing = jnp.logical_and(level == levels - 1, level > 1)
+        ahead_of_it = jnp.logical_and(level == levels - 2, level >= 1)
+        usual = jnp.logical_not(crossing)
 
         first[0][...] = own_ref[...] - low_ref[0] - high_ref[0]
         first[1][...] = broadening - low_ref[1] - high_ref[1]
@@ -367,7 +373,7 @@
             def _():
                 link_up(before, me - stride // 2).wait_recv()
 
-            @pl.when(has_high)
+            @pl.when(jnp.logical_and(has_high, usual))
             def _():
                 link_down(before, me + stride // 2).wait_recv()
 
@@ -382,13 +388,23 @@
             low = (from_low[before, 0], from_low[before, 1])
             low = dot(beside((weight_low[0], weight_low[1])), square(low))
             keep(link_low.at[level], low, -1.0)
-            high = (from_high[before, 0], from_high[before, 1])
-            high = dot(beside((weight_high[0], weight_high[1])), square(high))
-            keep(link_high.at[level], high, -1.0)
+
+            @pl.when(usual)
+            def _():
+                high = (from_high[before, 0], from_high[before, 1])
+                high = dot(beside((weight_high[0], weight_high[1])), square(high))
+                keep(link_high.at[level], high, -1.0)
+
+            @pl.when(jnp.logical_and(crossing, has_low))
+            def _():
+                cross_down(level, me - stride).start()
 
         @pl.when(inner)
         def _():
             link_up(level, me + stride).start()
+
+        @pl.when(jnp.logical_and(inner, jnp.logical_not(jnp.logical_or(crossing, ahead_of_it))))
+        def _():
             link_down(level, me - stride).start()
 
         @pl.when(level == levels)
@@ -405,14 +421,49 @@
         def _():
             pack_down(level, me + stride).wait_recv()
 
-        low = (link_low[level, 0], link_low[level, 1])
-        high = (link_high[level, 0], link_high[level, 1])
-        low_weight = dot(beside(low), square(unpacked(packed_low.at[level], row, col)))
-        high_weight = dot(beside(high), square(unpacked(packed_high.at[level], row, col)))
-        keep(weight_low, low_weight)
-        keep(weight_high, high_weight)
-        add(low_ref, dot(low_weight, square_t(low), transpose_b=True))
-        add(high_ref, dot(high_weight, square_t(high), transpose_b=True))
+        def weighed(link, arrived):
+            return dot(beside(link), square(unpacked(arrived, row, col)))
+
+        def gained(weight, link):
+            return dot(weight, square_t(link), transpose_b=True)
+
+        @pl.when(usual)
+        def _():
+            low = (link_low[level, 0], link_low[level, 1])
+            high = (link_high[level, 0], link_high[level, 1])
+            low_weight = weighed(low, packed_low.at[level])
+            high_weight = weighed(high, packed_high.at[level])
+            keep(weight_low, low_weight)
+            keep(weight_high, high_weight)
+            add(low_ref, gained(low_weight, low))
+            add(high_ref, gained(high_weight, high))
+
+        @pl.when(crossing)
+        def _():
+            low = (link_low[level, 0], link_low[level, 1])
+            low_weight = weighed(low, packed_low.at[level])
+            keep(weight_low, low_weight)
+            add(low_ref, gained(low_weight, low))
+
+            @pl.when(has_high)
+            def _():
+                cross_down(level, me + stride).wait_recv()
+
+            @pl.when(jnp.logical_not(has_high))
+            def _():
+                crossed[...] = jnp.zeros((2, n, n), F32)
+
+            high = (crossed[0].T, crossed[1].T)
+            link_high[level, 0] = high[0]
+            link_high[level, 1] = high[1]
+            high_weight = weighed(high, packed_high.at[level])
+            keep(weight_high, high_weight)
+            add(high_ref, gained(high_weight, high))
+
+            @pl.when(inner)
+            def _():
+                link_down(level, me - stride).start()
+
         return stride * 2
 
     lax.fori_loop(1, levels + 1, level_step, 1)
@@ -476,10 +527,21 @@
         def _():
             pack_down(level, me - stride).wait_send()
 
-        @pl.when(jnp.logical_and(has_low, has_high))
+        crossing = jnp.logical_and(level == levels - 1, level > 1)
+        ahead_of_it = jnp.logical_and(level == levels - 2, level >= 1)
+        inner = jnp.logical_and(has_low, has_high)
+
+        @pl.when(inner)
         def _():
             link_up(level, me + stride).wait_send()
+
+        @pl.when(jnp.logical_and(inner, jnp.logical_not(ahead_of_it)))
+        def _():
             link_down(level, me - stride).wait_send()
+
+        @pl.when(jnp.logical_and(crossing, has_low))
+        def _():
+            cross_down(level, me - stride).wait_send()
 
         return stride * 2
 
@@ -518,6 +580,8 @@
                 pltpu.VMEM((2, n, n), F32),
                 pack_shape, pack_shape, pack_shape,
                 link_shape, link_shape, link_shape, link_shape,
+                pltpu.VMEM((2, n, n), F32),
+                pltpu.SemaphoreType.DMA((2,)),
             ]
             + [sems] * 8,
             compiler_params=pltpu.CompilerParams(

time: 121 us -> 117 us (0.967); the launches traced: 121 us -> 115 us
  Pallas kernels: 116 us -> 110 us
    pallas_call x1, Pallas kernels: 116 us -> 110 us  [shards(): pl.pallas_call(functools.partial(kernel, count), out_shape=(pair, pair),...]
where the time goes in v6:
time: 117 us; the launch traced here: 115 us
  Pallas kernels  110 us (94%)
  local copies, waits for them, and re-layouts  3.12 us (3%)
  between operations  2 us (2%)
    pallas_call x1, Pallas kernels, shards(): pl.pallas_call(functools.partial(kernel, count), out_shape=(pair, pair),...  110 us
    unnamed x10, local copies, waits for them, and re-layouts  3.12 us

profile of v6, /device:TPU:34, one launch (start us, length us, event | category | flops | bytes accessed | tf_op | source)
XLA Modules:
  0.0 115.2 jit_solution(6442326393398009375)
XLA Ops:
  0.6 0.0 copy-start.3
  1.3 0.0 copy-start.2
  2.0 0.0 copy-done.3
  2.0 0.0 copy-done.2
  2.0 0.0 copy-start
  2.0 0.9 copy-done
  2.9 0.0 copy-start.1
  2.9 0.9 copy-done.1
  3.8 110.1 %shard_map.77 = (f32[2,128,128]{2,1,0:T(8,128)S(1)}, f32[2,128,128]{2,1,0:T(8,128)S(1)}) custom-call(f32[2,128]{1,0:T(2,128)S(1)} %copy-done.2, f32[2,128,128]{2,1,0:T(8,128)S(1)} %copy-done, f32[2,128]{1,0:T(2,128)S(1)} %copy-done.3, f32[2,128,128]{2,1,0:T(8,128)S(1)} %copy-done.1, f32[1]{0:T(128)S(6)} %copy.10.energy_ref, f32[1]{0:T(128)S(6)} %copy.11.broadening_ref), custom_call_target="tpu_custom_call" | custom-call | tf_op jit(solution)/shard_map/pallas_call | solution.py:563
  113.9 0.7 copy.12
  114.6 0.7 copy.13
Async XLA Ops:
  0.6 1.3 %copy-start.3 = (f32[2,128]{1,0:T(2,128)S(1)}, f32[2,128]{1,0:T(2,128)}, u32[]{:S(2)}) copy-start(f32[2,128]{1,0:T(2,128)} %strength_hbm.1) | copy-start | bytes 3076
  1.3 0.7 copy-start.2
  2.0 0.9 copy-start
  2.9 0.9 copy-start.1

commit v7 on v6

--- a/solution.py
+++ b/solution.py
@@ -291,7 +291,6 @@
     mine = coupling(strength_ref, hopping_ref, 0)
     next_one = jnp.where(me < count - 1, coupling(strength_ref, hopping_ref, 1), 0.0)
 
-    own_ref[...] = onsite(0)
     first[0][...] = onsite(1)
     first[1][...] = broadening
     invert((first,))
@@ -319,6 +318,7 @@
         from_low[0] = jnp.zeros((2, n, n), F32)
         packed_low[0] = jnp.zeros((n + STRIP, n), F32)
 
+    own_ref[...] = onsite(0)
     weight = dot(mine, inverse)
     keep(high_ref, side_by_side(dot(stacked(weight), mine, transpose_b=True)))
     keep(link_high.at[1], side_by_side(dot(stacked(weight), next_one)), -1.0)
@@ -473,38 +473,41 @@
     first[1][...] = broadening - jnp.where(upper, low_ref[1], high_ref[1])
     invert((first,))
     pack(last, [jnp.where(upper, spare[c], work[c]) for c in (0, 1)])
+    @pl.when(me >= 1)
+    def _():
+        pack_down(last, me - 1).start()
+
     left = [jnp.where(upper, work[c], spare[c]) for c in (0, 1)]
     left = [0.5 * (value + value.T) for value in left]
     keep(weight_low, beside(left))
 
-    @pl.when(me >= 1)
-    def _():
-        pack_down(last, me - 1).start()
-
     @pl.when(me + 1 >= count)
     def _():
         packed_high[last] = jnp.zeros((n + STRIP, n), F32)
 
-    first[0][...] = own_ref[...] - low_ref[0] - high_ref[0]
-    first[1][...] = broadening - low_ref[1] - high_ref[1]
+    weight = dot(mine.T, beside((weight_low[0], weight_low[1])))
+    keep(weight_high, weight)
+    below = dot(stacked(weight), mine)
+    second[0][...] = onsite(1) - below[:n]
+    second[1][...] = broadening - below[n:]
+
+    @pl.when(me + 1 < count)
+    def _():
+        pack_down(last, me + 1).wait_recv()
+
+    weight = dot(next_one, beside(unpacked(packed_high.at[last], row, col)))
+    above = dot(stacked(weight), next_one, transpose_b=True)
+    first[0][...] = second[0][...] - above[:n]
+    first[1][...] = second[1][...] - above[n:]
     invert((first,))
-    real_ref[0] = first[0][...]
-    imag_ref[0] = first[1][...]
-
-    weight = halves(dot(mine.T, beside((weight_low[0], weight_low[1]))))
-    below = dot(jnp.concatenate([weight[0], weight[1]], axis=0), mine)
-
-    @pl.when(me + 1 < count)
-    def _():
-        pack_down(last, me + 1).wait_recv()
-
-    weight = halves(dot(next_one, beside(unpacked(packed_high.at[last], row, col))))
-    above = dot(jnp.concatenate([weight[0], weight[1]], axis=0), next_one, transpose_b=True)
-    first[0][...] = onsite(1) - below[:n] - above[:n]
-    first[1][...] = broadening - below[n:] - above[n:]
-    invert((first,))
-    real_ref[1] = first[0][...]
-    imag_ref[1] = first[1][...]
+    result = (first[0][...], first[1][...])
+    real_ref[1] = result[0]
+    imag_ref[1] = result[1]
+    seen = (weight_high[0], weight_high[1])
+    term = cdot((seen[0].T, seen[1].T), result)
+    term = cdot(term, seen)
+    real_ref[0] = weight_low[0] + term[0]
+    imag_ref[0] = weight_low[1] + term[1]
 
     @pl.when(me + 1 < count)
     def _():

time: 117 us -> 116 us (level)
    pallas_call x1, Pallas kernels: 110 us -> 109 us  [shards(): pl.pallas_call(functools.partial(kernel, count), out_shape=(pair, pair),...]
where the time goes in v7:
time: 116 us; the launch traced here: 114 us
  Pallas kernels  109 us (94%)
  local copies, waits for them, and re-layouts  3.12 us (3%)
  between operations  2 us (2%)
    pallas_call x1, Pallas kernels, shards(): pl.pallas_call(functools.partial(kernel, count), out_shape=(pair, pair),...  109 us
    unnamed x10, local copies, waits for them, and re-layouts  3.12 us

profile of v7, /device:TPU:34, one launch (start us, length us, event | category | flops | bytes accessed | tf_op | source)
XLA Modules:
  0.0 114.0 jit_solution(8928173238028320403)
XLA Ops:
  0.6 0.0 copy-start.3
  1.3 0.0 copy-start.2
  2.0 0.0 copy-done.3
  2.0 0.0 copy-done.2
  2.0 0.0 copy-start
  2.0 0.9 copy-done
  2.9 0.0 copy-start.1
  2.9 0.9 copy-done.1
  3.8 108.9 %shard_map.77 = (f32[2,128,128]{2,1,0:T(8,128)S(1)}, f32[2,128,128]{2,1,0:T(8,128)S(1)}) custom-call(f32[2,128]{1,0:T(2,128)S(1)} %copy-done.2, f32[2,128,128]{2,1,0:T(8,128)S(1)} %copy-done, f32[2,128]{1,0:T(2,128)S(1)} %copy-done.3, f32[2,128,128]{2,1,0:T(8,128)S(1)} %copy-done.1, f32[1]{0:T(128)S(6)} %copy.10.energy_ref, f32[1]{0:T(128)S(6)} %copy.11.broadening_ref), custom_call_target="tpu_custom_call" | custom-call | tf_op jit(solution)/shard_map/pallas_call | solution.py:566
  112.7 0.7 copy.12
  113.4 0.7 copy.13
Async XLA Ops:
  0.6 1.3 %copy-start.3 = (f32[2,128]{1,0:T(2,128)S(1)}, f32[2,128]{1,0:T(2,128)}, u32[]{:S(2)}) copy-start(f32[2,128]{1,0:T(2,128)} %strength_hbm.1) | copy-start | bytes 3076
  1.3 0.7 copy-start.2
  2.0 0.9 copy-start
  2.9 0.9 copy-start.1

commit v8 on v7

--- a/solution.py
+++ b/solution.py
@@ -427,7 +427,17 @@
         def gained(weight, link):
             return dot(weight, square_t(link), transpose_b=True)
 
-        @pl.when(usual)
+        @pl.when(jnp.logical_and(level == levels, has_low))
+        def _():
+            low = (link_low[level, 0], link_low[level, 1])
+            add(low_ref, gained(weighed(low, packed_low.at[level]), low))
+
+        @pl.when(jnp.logical_and(level == levels, has_high))
+        def _():
+            high = (link_high[level, 0], link_high[level, 1])
+            add(high_ref, gained(weighed(high, packed_high.at[level]), high))
+
+        @pl.when(jnp.logical_and(usual, level < levels))
         def _():
             low = (link_low[level, 0], link_low[level, 1])
             high = (link_high[level, 0], link_high[level, 1])

time: 116 us -> 116 us (level)
  no operation moved by 1% of the time
where the time goes in v8:
time: 116 us; the launch traced here: 114 us
  Pallas kernels  109 us (94%)
  local copies, waits for them, and re-layouts  3.12 us (3%)
  between operations  2 us (2%)
    pallas_call x1, Pallas kernels, shards(): pl.pallas_call(functools.partial(kernel, count), out_shape=(pair, pair),...  109 us
    unnamed x10, local copies, waits for them, and re-layouts  3.12 us

profile of v8, /device:TPU:34, one launch (start us, length us, event | category | flops | bytes accessed | tf_op | source)
XLA Modules:
  0.0 113.8 jit_solution(13127006047085223652)
XLA Ops:
  0.6 0.0 copy-start.3
  1.3 0.0 copy-start.2
  2.0 0.0 copy-done.3
  2.0 0.0 copy-done.2
  2.0 0.0 copy-start
  2.0 0.9 copy-done
  2.9 0.0 copy-start.1
  2.9 0.9 copy-done.1
  3.8 108.7 %shard_map.77 = (f32[2,128,128]{2,1,0:T(8,128)S(1)}, f32[2,128,128]{2,1,0:T(8,128)S(1)}) custom-call(f32[2,128]{1,0:T(2,128)S(1)} %copy-done.2, f32[2,128,128]{2,1,0:T(8,128)S(1)} %copy-done, f32[2,128]{1,0:T(2,128)S(1)} %copy-done.3, f32[2,128,128]{2,1,0:T(8,128)S(1)} %copy-done.1, f32[1]{0:T(128)S(6)} %copy.10.energy_ref, f32[1]{0:T(128)S(6)} %copy.11.broadening_ref), custom_call_target="tpu_custom_call" | custom-call | tf_op jit(solution)/shard_map/pallas_call | solution.py:576
  112.5 0.7 copy.12
  113.2 0.7 copy.13
Async XLA Ops:
  0.6 1.3 %copy-start.3 = (f32[2,128]{1,0:T(2,128)S(1)}, f32[2,128]{1,0:T(2,128)}, u32[]{:S(2)}) copy-start(f32[2,128]{1,0:T(2,128)} %strength_hbm.1) | copy-start | bytes 3076
  1.3 0.7 copy-start.2
  2.0 0.9 copy-start
  2.9 0.9 copy-start.1
